TPU v7x, 32 devices: a whole 2x2x4 slice. The times are simulated.
32 devices in a mesh: depth: 4 (over z), imgx: 4 (over y, core), imgy: 2 (over x).
Axes of the slice: x: 2, y: 2, z: 4, core: 2. Of those that a mesh axis runs over, the one named last changes fastest.
Arguments:
- emissivity: bfloat16 [32, 512, 256], P('depth', 'imgx', 'imgy'), may hold values from 0.099609375 to 10
- bin_index: int32 [32, 512, 256], P('depth', 'imgx', 'imgy'), may hold values from 0 to 127
- color_table: bfloat16 [4, 128], replicated, may hold values from 0.049804688 to 1
- brick_order: int32 [4], replicated, may hold values from 0 to 3, each once
Outputs:
- image: float32 [4, 512, 256], P(None, 'imgx', 'imgy')
Inputs may be any that keep to these rules, and one draw needn't show every extreme that they name: brick_order names every brick index once.
All inputs are finite; a program needn't handle non-finite values.
Results may differ from a plain program's by a relative error of at most 0.0003.
Values sent between devices are 32-bit elements; how exact they have to be, the bound alone decides.
A program may use at most 64 MiB of HBM per device.

v0:
```python
import functools

import jax
import jax.numpy as jnp
from jax import lax
from jax.experimental import pallas as pl
from jax.experimental.pallas import tpu as pltpu
from jax.sharding import PartitionSpec as P

MESH = pl.DeviceIdType.MESH
BLOCK = 16
LANES = 128


def look(channel_tables, bins):
    slabs = len(channel_tables[0])
    if slabs == 1:
        return [jnp.take_along_axis(t[0], bins, axis=1, mode="promise_in_bounds") for t in channel_tables]
    within = bins % LANES
    slab_of = bins // LANES
    out = []
    for t in channel_tables:
        value = jnp.take_along_axis(t[0], within, axis=1, mode="promise_in_bounds")
        for s in range(1, slabs):
            other = jnp.take_along_axis(t[s], within, axis=1, mode="promise_in_bounds")
            value = jnp.where(slab_of == s, other, value)
        out.append(value)
    return out


def scaled_tables(table_ref, ray_step):
    table = table_ref[...].astype(jnp.float32) * ray_step
    slabs = table.shape[1] // LANES
    return [
        [jnp.broadcast_to(table[c : c + 1, s * LANES : (s + 1) * LANES], (BLOCK, LANES)) for s in range(slabs)]
        for c in range(4)
    ]


def march(tables, emis_ref, bins_ref, start):
    cells = emis_ref.shape[0]
    rows = pl.ds(start, BLOCK)
    color = [None] * 3
    depth_in = None
    for z in range(cells):
        bright = emis_ref[z, rows, :].astype(jnp.float32)
        looked = look(tables, bins_ref[z, rows, :])
        rate = bright * looked[3]
        if depth_in is None:
            color = [bright * looked[c] for c in range(3)]
            depth_in = rate
        else:
            seen = bright * jnp.exp(-depth_in)
            color = [color[c] + seen * looked[c] for c in range(3)]
            depth_in = depth_in + rate
    return color + [jnp.exp(-depth_in)]


def fused(n, ray_step, emis_hbm, bins_hbm, table_ref, order_ref, out_ref,
          emis, bins, outgoing, arrived, mine, in_sem, send_sem, recv_sem, give_sem, take_sem):
    me = lax.axis_index("depth")
    rows = mine.shape[1]
    hops = sorted(range(1, n), key=lambda h: min(h, n - h)) + [0]

    def at_hop(h):
        return lax.rem(me + h, n)

    def span(d):
        return pl.ds(pl.multiple_of(d * rows, BLOCK), rows)

    loads = []
    for i, h in enumerate(hops):
        dest = span(at_hop(h))
        pair = (
            pltpu.make_async_copy(emis_hbm.at[:, dest, :], emis.at[i], in_sem.at[2 * i]),
            pltpu.make_async_copy(bins_hbm.at[:, dest, :], bins.at[i], in_sem.at[2 * i + 1]),
        )
        for c in pair:
            c.start()
        loads.append(pair)

    barrier = pltpu.get_barrier_semaphore()
    for h in range(1, n):
        pl.semaphore_signal(barrier, inc=1, device_id={"depth": at_hop(h)}, device_id_type=MESH)

    tables = scaled_tables(table_ref, ray_step)
    sends = []
    for i, h in enumerate(hops):
        for c in loads[i]:
            c.wait()
        for r in range(0, rows, BLOCK):
            part = march(tables, emis.at[i], bins.at[i], r)
            for c in range(4):
                if h == 0:
                    arrived[me, c, pl.ds(r, BLOCK), :] = part[c]
                else:
                    outgoing[i, c, pl.ds(r, BLOCK), :] = part[c]
        if h != 0:
            if i == 0:
                pl.semaphore_wait(barrier, n - 1)
            copy = pltpu.make_async_remote_copy(
                src_ref=outgoing.at[i],
                dst_ref=arrived.at[me],
                send_sem=send_sem.at[i],
                recv_sem=recv_sem.at[i],
                device_id={"depth": at_hop(h)},
                device_id_type=MESH,
            )
            copy.start()
            sends.append(copy)
    for copy in sends:
        copy.wait_recv()

    for r in range(0, rows, BLOCK):
        at = pl.ds(r, BLOCK)
        first = order_ref[0]
        color = [arrived[first, c, at, :] for c in range(3)]
        through = arrived[first, 3, at, :]
        for k in range(1, n):
            b = order_ref[k]
            color = [color[c] + through * arrived[b, c, at, :] for c in range(3)]
            through = through * arrived[b, 3, at, :]
        for c in range(3):
            mine[c, at, :] = color[c]
        mine[3, at, :] = 1.0 - through

    gives = []
    for i, h in enumerate(hops[:-1]):
        copy = pltpu.make_async_remote_copy(
            src_ref=mine,
            dst_ref=out_ref.at[:, span(me), :],
            send_sem=give_sem.at[i],
            recv_sem=take_sem.at[i],
            device_id={"depth": at_hop(h)},
            device_id_type=MESH,
        )
        copy.start()
        gives.append(copy)
    out_ref[:, span(me), :] = mine[...]
    for copy in sends:
        copy.wait_send()
    for copy in gives:
        copy.wait()


def fused_call(emissivity, bin_index, color_table, brick_order, n, ray_step):
    cells, cols_x, cols_y = emissivity.shape
    rows = cols_x // n
    return pl.pallas_call(
        functools.partial(fused, n, ray_step),
        out_shape=pltpu.VMEM((4, cols_x, cols_y), jnp.float32),
        in_specs=[
            pl.BlockSpec(memory_space=pltpu.HBM),
            pl.BlockSpec(memory_space=pltpu.HBM),
            pl.BlockSpec(memory_space=pltpu.VMEM),
            pl.BlockSpec(memory_space=pltpu.SMEM),
        ],
        out_specs=pl.BlockSpec(memory_space=pltpu.VMEM),
        scratch_shapes=[
            pltpu.VMEM((n, cells, rows, cols_y), jnp.bfloat16),
            pltpu.VMEM((n, cells, rows, cols_y), jnp.int32),
            pltpu.VMEM((n - 1, 4, rows, cols_y), jnp.float32),
            pltpu.VMEM((n, 4, rows, cols_y), jnp.float32),
            pltpu.VMEM((4, rows, cols_y), jnp.float32),
            pltpu.SemaphoreType.DMA((2 * n,)),
            pltpu.SemaphoreType.DMA((n - 1,)),
            pltpu.SemaphoreType.DMA((n - 1,)),
            pltpu.SemaphoreType.DMA((n - 1,)),
            pltpu.SemaphoreType.DMA((n - 1,)),
        ],
        compiler_params=pltpu.CompilerParams(collective_id=0, has_side_effects=True),
    )(emissivity, bin_index, color_table, brick_order)


def march_kernel(ray_step, emis_ref, bins_ref, table_ref, out_ref):
    tables = scaled_tables(table_ref, ray_step)

    @pl.loop(0, emis_ref.shape[1] // BLOCK)
    def _(r):
        start = pl.multiple_of(r * BLOCK, BLOCK)
        part = march(tables, emis_ref, bins_ref, start)
        for c in range(4):
            out_ref[c, pl.ds(start, BLOCK), :] = part[c]


def spread(emissivity, bin_index, color_table, brick_order, n, ray_step):
    cells, cols_x, cols_y = emissivity.shape
    piece_len = cols_x * cols_y // n
    stacked = pl.pallas_call(
        functools.partial(march_kernel, ray_step),
        out_shape=jax.ShapeDtypeStruct((4, cols_x, cols_y), jnp.float32),
        in_specs=[pl.BlockSpec(memory_space=pltpu.VMEM)] * 3,
        out_specs=pl.BlockSpec(memory_space=pltpu.VMEM),
    )(emissivity, bin_index, color_table)
    stacked = stacked.reshape(1, 4, n, piece_len).transpose(2, 0, 1, 3).reshape(n, 4, piece_len)
    received = lax.all_to_all(stacked, "depth", split_axis=0, concat_axis=0, tiled=True)
    ordered = jnp.take(received, brick_order, axis=0)
    color, through = ordered[0, 0:3], ordered[0, 3]
    for k in range(1, n):
        color = color + through * ordered[k, 0:3]
        through = through * ordered[k, 3]
    piece = jnp.concatenate([color, (1.0 - through)[None]], 0)
    return lax.all_gather(piece, "depth", axis=1, tiled=True).reshape(4, cols_x, cols_y)


def on_device(emissivity, bin_index, color_table, brick_order):
    cells, cols_x, cols_y = emissivity.shape
    n = lax.axis_size("depth")
    ray_step = 2.0 / (cells * n)
    piecewise = cols_x % (n * BLOCK) == 0
    form = fused_call if piecewise else spread
    return form(emissivity, bin_index, color_table, brick_order, n, ray_step)


def solution(mesh):
    return jax.shard_map(
        on_device,
        mesh=mesh,
        in_specs=(P("depth", "imgx", "imgy"), P("depth", "imgx", "imgy"), P(), P()),
        out_specs=P(None, "imgx", "imgy"),
        check_vma=False,
    )
```

profile of v0, /device:TPU:0, one launch (start us, length us, event | category | flops | bytes accessed | tf_op | source)
XLA Modules:
  0.0 18.7 jit_solution(5153895780417804144)
XLA Ops:
  0.0 18.0 %shard_map.46 = f32[4,128,128]{2,1,0:T(8,128)S(1)} custom-call(bf16[8,128,128]{2,1,0:T(8,128)(2,1)} %emis_hbm.1, s32[8,128,128]{2,1,0:T(8,128)} %bins_hbm.1, bf16[4,128]{1,0:T(4,128)(2,1)} %table_ref.1, s32[4]{0:T(128)} %order_ref.1), custom_call_target="tpu_custom_call" | custom-call | tf_op jit(solution)/shard_map/pallas_call | solution.py:149
  18.0 0.7 %copy.6 = f32[4,128,128]{2,1,0:T(8,128)} copy(f32[4,128,128]{2,1,0:T(8,128)S(1)} %shard_map.46) | data formatting | bytes 524288
where the time goes:
time: 18.8 us; the launch traced here: 18.7 us
  Pallas kernels  18 us (96%)
  local copies, waits for them, and re-layouts  0.71 us (4%)
    pallas_call x1, Pallas kernels, fused_call(): pl.pallas_call(functools.partial(fused, n, ray_step), out_shape=pltpu.VME...  18 us
    unnamed x1, local copies, waits for them, and re-layouts  0.71 us

commit v1 on v0

v1 whole, which is shorter than its diff:
```python
import functools

import jax
import jax.numpy as jnp
from jax import lax
from jax.experimental import pallas as pl
from jax.experimental.pallas import tpu as pltpu
from jax.sharding import PartitionSpec as P

MESH = pl.DeviceIdType.MESH
BLOCK = 8
LANES = 128
GROUP = 4
RS = (((3,), (2,), (1,), (0,)), ((3,), (2,), (0,), (1,)), ((0, 1), (3,), (2,)), ((0, 1), (2,), (3,)))
RELAY_ORDER = ((3, 0), (2, 1))
DIRECT = (2,)


def look(channel_tables, bins):
    slabs = len(channel_tables[0])
    if slabs == 1:
        return [jnp.take_along_axis(t[0], bins, axis=1, mode="promise_in_bounds") for t in channel_tables]
    within = bins % LANES
    slab_of = bins // LANES
    out = []
    for t in channel_tables:
        value = jnp.take_along_axis(t[0], within, axis=1, mode="promise_in_bounds")
        for s in range(1, slabs):
            other = jnp.take_along_axis(t[s], within, axis=1, mode="promise_in_bounds")
            value = jnp.where(slab_of == s, other, value)
        out.append(value)
    return out


def scaled_tables(table_ref, ray_step):
    table = table_ref[...].astype(jnp.float32) * ray_step
    slabs = table.shape[1] // LANES
    return [
        [jnp.broadcast_to(table[c : c + 1, s * LANES : (s + 1) * LANES], (BLOCK, LANES)) for s in range(slabs)]
        for c in range(4)
    ]


def march(tables, emis_ref, bins_ref, start):
    cells = emis_ref.shape[0]
    rows = pl.ds(start, BLOCK)
    color = [None] * 3
    depth_in = None
    for z in range(cells):
        bright = emis_ref[z, rows, :].astype(jnp.float32)
        looked = look(tables, bins_ref[z, rows, :])
        rate = bright * looked[3]
        if depth_in is None:
            color = [bright * looked[c] for c in range(3)]
            depth_in = rate
        else:
            seen = bright * jnp.exp(-depth_in)
            color = [color[c] + seen * looked[c] for c in range(3)]
            depth_in = depth_in + rate
    return color + [jnp.exp(-depth_in)]


def pick(options, me):
    value = jnp.int32(options[0])
    for i in range(1, len(options)):
        value = jnp.where(me == i, jnp.int32(options[i]), value)
    return value


def owned_sizes(blocks):
    quarter, shift = blocks // 4, blocks // 16
    return (quarter, quarter, quarter + shift, quarter - shift)


def owned_blocks(sizes, groups):
    steps = []
    for group in groups:
        woven = [((k + 0.5) / sizes[o], i, o, k) for i, o in enumerate(group) for k in range(sizes[o])]
        steps += [(o, k) for _, _, o, k in sorted(woven)]
    return steps


def either(me, members):
    return functools.reduce(jnp.logical_or, [me == m for m in members], False)


def fused(n, ray_step, emis_hbm, bins_hbm, table_in, order_in, out_ref,
          emis, bins, outgoing, arrived, mine, table_v, order_s, in_sem, aux_sem,
          send_sem, recv_sem, give_sem, take_sem, cross_sem, relay_sem, ready_sem):
    me = lax.axis_index("depth")
    y = lax.axis_index("imgx")
    core = lax.rem(y, 2)
    leaf, hub = core == 0, core == 1
    leaf_y, hub_y = y - core, y - core + 1
    blocks = emis.shape[0]
    half = n // 2
    sizes = owned_sizes(blocks)
    offs = [sum(sizes[:m]) for m in range(n)]
    plan = [owned_blocks(sizes, RS[m]) for m in range(n)]

    def at_leaf(d):
        return {"depth": d, "imgx": leaf_y}

    def at_hub(d):
        return {"depth": d, "imgx": hub_y}

    barrier = pltpu.get_barrier_semaphore()

    @pl.when(hub)
    def _():
        for h in range(1, n):
            pl.semaphore_signal(barrier, inc=1, device_id=at_hub(lax.rem(me + h, n)), device_id_type=MESH)
        for h in range(n):
            pl.semaphore_signal(barrier, inc=1, device_id=at_leaf(lax.rem(me + h, n)), device_id_type=MESH)

    def block_rows(block):
        return pl.ds(pl.multiple_of(block * BLOCK, BLOCK), BLOCK)

    owner = [pick([plan[m][q][0] for m in range(n)], me) for q in range(blocks)]
    place = [pick([plan[m][q][1] for m in range(n)], me) for q in range(blocks)]
    block = [pick([offs[plan[m][q][0]] + plan[m][q][1] for m in range(n)], me) for q in range(blocks)]
    first_own = pick(offs, me)
    group = blocks // GROUP

    for q in range(blocks):
        src = block_rows(block[q])
        pltpu.make_async_copy(emis_hbm.at[:, src, :], emis.at[q], in_sem.at[0, q // group]).start()
        pltpu.make_async_copy(bins_hbm.at[:, src, :], bins.at[q], in_sem.at[1, q // group]).start()
        if q == group - 1:
            tc = pltpu.make_async_copy(table_in, table_v, aux_sem.at[0])
            oc = pltpu.make_async_copy(order_in, order_s, aux_sem.at[1])
            tc.start()
            oc.start()
    tc.wait()
    tables = scaled_tables(table_v, ray_step)

    def ship(q):
        pltpu.make_async_remote_copy(
            src_ref=outgoing.at[q],
            dst_ref=arrived.at[core, place[q], me],
            send_sem=send_sem,
            recv_sem=recv_sem.at[core, place[q]],
            device_id=at_hub(owner[q]),
            device_id_type=MESH,
        ).start()

    for q in range(blocks):
        if q % group == 0:
            part = pl.ds(q, group)
            pltpu.make_async_copy(emis.at[part], emis.at[part], in_sem.at[0, q // group]).wait()
            pltpu.make_async_copy(bins.at[part], bins.at[part], in_sem.at[1, q // group]).wait()
        got = march(tables, emis.at[q], bins.at[q], 0)
        for c in range(4):
            outgoing[q, c, :, :] = got[c]
        if q == 0:
            pl.semaphore_wait(barrier, jnp.where(hub, n - 1, n))

            @pl.when(leaf)
            def _():
                for h in range(n):
                    pl.semaphore_signal(ready_sem, inc=1, device_id=at_hub(lax.rem(me + h, n)), device_id_type=MESH)
        stays = [m for m in range(n) if plan[m][q][0] == m]
        if not stays:
            ship(q)
        else:
            here = jnp.logical_and(hub, either(me, stays))

            @pl.when(here)
            def _():
                arrived[1, place[q], me] = outgoing[q]

            @pl.when(jnp.logical_not(here))
            def _():
                ship(q)

    oc.wait()
    own_count = pick(sizes, me)
    cross = jnp.where(me < half, half, 0)
    partner = me + 1 - 2 * lax.rem(me, 2)
    cross_slot = jnp.where(me < half, me, n - 1 - me)
    direct = either(me, DIRECT)

    def span_bytes(ref, sem, other):
        return pltpu.make_async_remote_copy(src_ref=ref, dst_ref=ref, send_sem=sem, recv_sem=other, device_id=at_hub(me), device_id_type=MESH)

    def give(k, tile, d, sem):
        pltpu.make_async_remote_copy(
            src_ref=mine.at[tile, k],
            dst_ref=out_ref.at[:, block_rows(first_own + k), :],
            send_sem=give_sem,
            recv_sem=sem,
            device_id=at_leaf(d) if tile == 0 else at_hub(d),
            device_id_type=MESH,
        ).start()

    @pl.when(hub)
    def _():
        pl.semaphore_wait(ready_sem, n)
        rank = [sum(jnp.where(order_s[q] == m, q, 0) for q in range(n)) for m in range(n)]
        before = [[rank[a] < rank[b] for b in range(n)] for a in range(n)]

        def settle(k, tile):
            span_bytes(arrived.at[tile, 0, pl.ds(0, n - tile)], send_sem, recv_sem.at[tile, k]).wait_recv()
            passed = [arrived[tile, k, m, 3] for m in range(n)]
            through = functools.reduce(lambda u, v: u * v, passed)
            color = [0.0] * 3
            for b in range(n):
                ahead = None
                for a in range(n):
                    if a != b:
                        factor = jnp.where(before[a][b], passed[a], 1.0)
                        ahead = factor if ahead is None else ahead * factor
                color = [color[c] + ahead * arrived[tile, k, b, c] for c in range(3)]
            for c in range(3):
                mine[tile, k, c] = color[c]
            mine[tile, k, 3] = 1.0 - through

        def chunk(k, carry):
            for tile in range(2):
                settle(k, tile)
                give(k, tile, cross, cross_sem.at[cross_slot, k])
                give(k, tile, partner, take_sem)
                if tile == 0:
                    give(k, tile, me, take_sem)
            return carry

        lax.fori_loop(0, own_count, chunk, 0)
        if DIRECT:
            @pl.when(direct)
            def _():
                def more(k, carry):
                    for tile in range(2):
                        give(k, tile, cross + 1, take_sem)
                    return carry
                lax.fori_loop(0, own_count, more, 0)

        def keep(k, carry):
            out_ref[:, block_rows(first_own + k), :] = mine[1, k]
            return carry

        lax.fori_loop(0, own_count, keep, 0)

    even = lax.rem(me, 2) == 0

    @pl.when(even)
    def _():
        for left_far, right_far in RELAY_ORDER:
            both = (left_far, right_far)
            far = pick([left_far] * half + [right_far] * half, me)
            begin = pick([offs[left_far]] * half + [offs[right_far]] * half, me)
            count = pick([sizes[left_far]] * half + [sizes[right_far]] * half, me)
            slot = pick([n - 1 - left_far] * half + [right_far] * half, me)
            handed = [m for m in both if m not in DIRECT]

            def relay(k, carry):
                spot = out_ref.at[:, block_rows(begin + k), :]
                span_bytes(spot, relay_sem, cross_sem.at[slot, k]).wait_recv()

                @pl.when(either(far, handed))
                def _():
                    pltpu.make_async_remote_copy(
                        src_ref=spot, dst_ref=spot, send_sem=relay_sem, recv_sem=take_sem,
                        device_id={"depth": me + 1}, device_id_type=MESH).start()
                return carry

            lax.fori_loop(0, count, relay, 0)

    def rows_of(count):
        return out_ref.at[:, pl.ds(0, count * BLOCK), :]

    for m in range(n):
        cross_owners = [o for o in range(n) if (o < half) != (m < half)]
        near = [o for o in range(n) if (o < half) == (m < half)]
        into = near if m % 2 == 0 else list(range(n))
        with_direct = [o for o in cross_owners if m % 2 == 0 and o not in DIRECT]

        @pl.when(jnp.logical_and(me == m, leaf))
        def _():
            span_bytes(outgoing, send_sem, take_sem).wait_send()
            span_bytes(rows_of(sum(sizes[o] for o in into)), give_sem, take_sem).wait_recv()

        @pl.when(jnp.logical_and(me == m, hub))
        def _():
            span_bytes(outgoing.at[pl.ds(0, blocks - sizes[m])], send_sem, take_sem).wait_send()
            span_bytes(rows_of(sum(sizes[o] for o in into) - sizes[m]), give_sem, take_sem).wait_recv()
            for _ in range(7 if m in DIRECT else 5):
                span_bytes(rows_of(sizes[m]), give_sem, take_sem).wait_send()
        if with_direct:
            @pl.when(me == m)
            def _():
                span_bytes(rows_of(sum(sizes[o] for o in with_direct)), relay_sem, take_sem).wait_send()


def fused_call(emissivity, bin_index, color_table, brick_order, n, ray_step):
    cells, cols_x, cols_y = emissivity.shape
    blocks = cols_x // BLOCK
    most = max(owned_sizes(blocks))
    return pl.pallas_call(
        functools.partial(fused, n, ray_step),
        out_shape=pltpu.VMEM((4, cols_x, cols_y), jnp.float32),
        in_specs=[pl.BlockSpec(memory_space=pltpu.HBM)] * 4,
        out_specs=pl.BlockSpec(memory_space=pltpu.VMEM),
        scratch_shapes=[
            pltpu.VMEM((blocks, cells, BLOCK, cols_y), jnp.bfloat16),
            pltpu.VMEM((blocks, cells, BLOCK, cols_y), jnp.int32),
            pltpu.VMEM((blocks, 4, BLOCK, cols_y), jnp.float32),
            pltpu.VMEM((2, most, n, 4, BLOCK, cols_y), jnp.float32),
            pltpu.VMEM((2, most, 4, BLOCK, cols_y), jnp.float32),
            pltpu.VMEM(color_table.shape, color_table.dtype),
            pltpu.SMEM(brick_order.shape, brick_order.dtype),
            pltpu.SemaphoreType.DMA((2, GROUP)),
            pltpu.SemaphoreType.DMA((2,)),
            pltpu.SemaphoreType.DMA(()),
            pltpu.SemaphoreType.DMA((2, most)),
            pltpu.SemaphoreType.DMA(()),
            pltpu.SemaphoreType.DMA(()),
            pltpu.SemaphoreType.DMA((2, most)),
            pltpu.SemaphoreType.DMA(()),
            pltpu.SemaphoreType.REGULAR,
        ],
        compiler_params=pltpu.CompilerParams(collective_id=0, has_side_effects=True),
    )(emissivity, bin_index, color_table, brick_order)


def march_kernel(ray_step, emis_ref, bins_ref, table_ref, out_ref):
    tables = scaled_tables(table_ref, ray_step)

    @pl.loop(0, emis_ref.shape[1] // BLOCK)
    def _(r):
        start = pl.multiple_of(r * BLOCK, BLOCK)
        part = march(tables, emis_ref, bins_ref, start)
        for c in range(4):
            out_ref[c, pl.ds(start, BLOCK), :] = part[c]


def spread(emissivity, bin_index, color_table, brick_order, n, ray_step):
    cells, cols_x, cols_y = emissivity.shape
    piece_len = cols_x * cols_y // n
    stacked = pl.pallas_call(
        functools.partial(march_kernel, ray_step),
        out_shape=jax.ShapeDtypeStruct((4, cols_x, cols_y), jnp.float32),
        in_specs=[pl.BlockSpec(memory_space=pltpu.VMEM)] * 3,
        out_specs=pl.BlockSpec(memory_space=pltpu.VMEM),
    )(emissivity, bin_index, color_table)
    stacked = stacked.reshape(1, 4, n, piece_len).transpose(2, 0, 1, 3).reshape(n, 4, piece_len)
    received = lax.all_to_all(stacked, "depth", split_axis=0, concat_axis=0, tiled=True)
    ordered = jnp.take(received, brick_order, axis=0)
    color, through = ordered[0, 0:3], ordered[0, 3]
    for k in range(1, n):
        color = color + through * ordered[k, 0:3]
        through = through * ordered[k, 3]
    piece = jnp.concatenate([color, (1.0 - through)[None]], 0)
    return lax.all_gather(piece, "depth", axis=1, tiled=True).reshape(4, cols_x, cols_y)


def on_device(emissivity, bin_index, color_table, brick_order):
    cells, cols_x, cols_y = emissivity.shape
    n = lax.axis_size("depth")
    ray_step = 2.0 / (cells * n)
    paired = lax.axis_size("imgx") % 2 == 0
    piecewise = n == len(RS) and paired and cols_x % (4 * n * BLOCK) == 0
    form = fused_call if piecewise else spread
    return form(emissivity, bin_index, color_table, brick_order, n, ray_step)


def solution(mesh):
    return jax.shard_map(
        on_device,
        mesh=mesh,
        in_specs=(P("depth", "imgx", "imgy"), P("depth", "imgx", "imgy"), P(), P()),
        out_specs=P(None, "imgx", "imgy"),
        check_vma=False,
    )
```

time: 18.8 us -> 17 us (0.904)
  Pallas kernels: 18 us -> 16.1 us
    pallas_call x1, Pallas kernels: 18 us -> 16.1 us  [fused_call(): pl.pallas_call(functools.partial(fused, n, ray_step), out_shape=pltpu.VME...]
where the time goes in v1:
time: 17 us; the launch traced here: 16.8 us
  Pallas kernels  16.1 us (95%)
  local copies, waits for them, and re-layouts  0.71 us (4%)
    pallas_call x1, Pallas kernels, fused_call(): pl.pallas_call(functools.partial(fused, n, ray_step), out_shape=pltpu.VME...  16.1 us
    unnamed x1, local copies, waits for them, and re-layouts  0.71 us

profile of v1, /device:TPU:0, one launch (start us, length us, event | category | flops | bytes accessed | tf_op | source)
XLA Modules:
  0.0 16.8 jit_solution(9962344489010176637)
XLA Ops:
  0.0 16.1 %shard_map.46 = f32[4,128,128]{2,1,0:T(8,128)S(1)} custom-call(bf16[8,128,128]{2,1,0:T(8,128)(2,1)} %emis_hbm.1, s32[8,128,128]{2,1,0:T(8,128)} %bins_hbm.1, bf16[4,128]{1,0:T(4,128)(2,1)} %table_in.1, s32[4]{0:T(128)} %order_in.1), custom_call_target="tpu_custom_call" | custom-call | tf_op jit(solution)/shard_map/pallas_call | solution.py:298
  16.1 0.7 %copy.6 = f32[4,128,128]{2,1,0:T(8,128)} copy(f32[4,128,128]{2,1,0:T(8,128)S(1)} %shard_map.46) | data formatting | bytes 524288

commit v2 on v1

--- a/solution.py
+++ b/solution.py
@@ -10,10 +10,12 @@
 MESH = pl.DeviceIdType.MESH
 BLOCK = 8
 LANES = 128
+MEET = 12
 GROUP = 4
-RS = (((3,), (2,), (1,), (0,)), ((3,), (2,), (0,), (1,)), ((0, 1), (3,), (2,)), ((0, 1), (2,), (3,)))
+RS = (((1,), (2,), (3,), (0,)), ((0,), (2,), (3,), (1,)), ((0, 1), (3,), (2,)), ((2, 0, 1), (3,)))
 RELAY_ORDER = ((3, 0), (2, 1))
-DIRECT = (2,)
+DIRECT = (1, 1, 4, 0)
+SIZES = (4, 4, 8, 0)
 
 
 def look(channel_tables, bins):
@@ -67,9 +69,8 @@
     return value
 
 
-def owned_sizes(blocks):
-    quarter, shift = blocks // 4, blocks // 16
-    return (quarter, quarter, quarter + shift, quarter - shift)
+def scaled(shares, blocks):
+    return tuple(share * blocks // sum(SIZES) for share in shares)
 
 
 def owned_blocks(sizes, groups):
@@ -86,7 +87,7 @@
 
 def fused(n, ray_step, emis_hbm, bins_hbm, table_in, order_in, out_ref,
           emis, bins, outgoing, arrived, mine, table_v, order_s, in_sem, aux_sem,
-          send_sem, recv_sem, give_sem, take_sem, cross_sem, relay_sem, ready_sem):
+          send_sem, recv_sem, give_sem, take_sem, cross_sem, relay_sem, ready_sem, know_sem, leaf_sem):
     me = lax.axis_index("depth")
     y = lax.axis_index("imgx")
     core = lax.rem(y, 2)
@@ -94,7 +95,7 @@
     leaf_y, hub_y = y - core, y - core + 1
     blocks = emis.shape[0]
     half = n // 2
-    sizes = owned_sizes(blocks)
+    sizes, direct_of = scaled(SIZES, blocks), scaled(DIRECT, blocks)
     offs = [sum(sizes[:m]) for m in range(n)]
     plan = [owned_blocks(sizes, RS[m]) for m in range(n)]
 
@@ -108,10 +109,11 @@
 
     @pl.when(hub)
     def _():
-        for h in range(1, n):
-            pl.semaphore_signal(barrier, inc=1, device_id=at_hub(lax.rem(me + h, n)), device_id_type=MESH)
-        for h in range(n):
-            pl.semaphore_signal(barrier, inc=1, device_id=at_leaf(lax.rem(me + h, n)), device_id_type=MESH)
+        pl.semaphore_signal(barrier, inc=1, device_id=at_leaf(me), device_id_type=MESH)
+        for d in range(n):
+            @pl.when((d > me) | ((d == 0) & (me == 1)))
+            def _():
+                pl.semaphore_signal(barrier, inc=1, device_id=at_hub(d), device_id_type=MESH)
 
     def block_rows(block):
         return pl.ds(pl.multiple_of(block * BLOCK, BLOCK), BLOCK)
@@ -131,6 +133,34 @@
             oc = pltpu.make_async_copy(order_in, order_s, aux_sem.at[1])
             tc.start()
             oc.start()
+    pl.semaphore_wait(barrier, jnp.where(hub, jnp.maximum(me, 1), 1))
+
+    @pl.when(hub)
+    def _():
+        for d in range(n):
+            @pl.when(d < me)
+            def _():
+                pl.semaphore_signal(know_sem.at[me], inc=1, device_id=at_hub(d), device_id_type=MESH)
+        pl.semaphore_wait(leaf_sem, 1)
+        for d in range(n):
+            @pl.when(d < me)
+            def _():
+                pl.semaphore_signal(know_sem.at[d], inc=1, device_id=at_leaf(me), device_id_type=MESH)
+
+    @pl.when(leaf)
+    def _():
+        pl.semaphore_signal(leaf_sem, inc=1, device_id=at_hub(me), device_id_type=MESH)
+
+    def meet(t):
+        @pl.when(jnp.logical_and(hub, t > me))
+        def _():
+            pl.semaphore_wait(know_sem.at[t], 1)
+            pl.semaphore_signal(know_sem.at[t], inc=1, device_id=at_leaf(me), device_id_type=MESH)
+
+        @pl.when(jnp.logical_and(leaf, t != me))
+        def _():
+            pl.semaphore_wait(know_sem.at[t], 1)
+
     tc.wait()
     tables = scaled_tables(table_v, ray_step)
 
@@ -144,6 +174,7 @@
             device_id_type=MESH,
         ).start()
 
+    last_meet = blocks * MEET // sum(SIZES)
     for q in range(blocks):
         if q % group == 0:
             part = pl.ds(q, group)
@@ -152,9 +183,18 @@
         got = march(tables, emis.at[q], bins.at[q], 0)
         for c in range(4):
             outgoing[q, c, :, :] = got[c]
-        if q == 0:
-            pl.semaphore_wait(barrier, jnp.where(hub, n - 1, n))
-
+        fresh = [m for m in range(n) if plan[m][q][0] not in [o for o, _ in plan[m][:q]]]
+        if fresh:
+            @pl.when(either(me, fresh))
+            def _():
+                meet(owner[q])
+        if q == last_meet:
+            for t in range(n):
+                unmet = [m for m in range(n) if m != t and t not in [o for o, _ in plan[m]]]
+                if unmet:
+                    @pl.when(either(me, unmet))
+                    def _():
+                        meet(jnp.int32(t))
             @pl.when(leaf)
             def _():
                 for h in range(n):
@@ -178,7 +218,7 @@
     cross = jnp.where(me < half, half, 0)
     partner = me + 1 - 2 * lax.rem(me, 2)
     cross_slot = jnp.where(me < half, me, n - 1 - me)
-    direct = either(me, DIRECT)
+    direct = pick(direct_of, me)
 
     def span_bytes(ref, sem, other):
         return pltpu.make_async_remote_copy(src_ref=ref, dst_ref=ref, send_sem=sem, recv_sem=other, device_id=at_hub(me), device_id_type=MESH)
@@ -225,14 +265,12 @@
             return carry
 
         lax.fori_loop(0, own_count, chunk, 0)
-        if DIRECT:
-            @pl.when(direct)
-            def _():
-                def more(k, carry):
-                    for tile in range(2):
-                        give(k, tile, cross + 1, take_sem)
-                    return carry
-                lax.fori_loop(0, own_count, more, 0)
+        if any(direct_of):
+            def more(k, carry):
+                for tile in range(2):
+                    give(k, tile, cross + 1, take_sem)
+                return carry
+            lax.fori_loop(own_count - direct, own_count, more, 0)
 
         def keep(k, carry):
             out_ref[:, block_rows(first_own + k), :] = mine[1, k]
@@ -246,17 +284,16 @@
     def _():
         for left_far, right_far in RELAY_ORDER:
             both = (left_far, right_far)
-            far = pick([left_far] * half + [right_far] * half, me)
             begin = pick([offs[left_far]] * half + [offs[right_far]] * half, me)
             count = pick([sizes[left_far]] * half + [sizes[right_far]] * half, me)
             slot = pick([n - 1 - left_far] * half + [right_far] * half, me)
-            handed = [m for m in both if m not in DIRECT]
+            handed = count - pick([direct_of[left_far]] * half + [direct_of[right_far]] * half, me)
 
             def relay(k, carry):
                 spot = out_ref.at[:, block_rows(begin + k), :]
                 span_bytes(spot, relay_sem, cross_sem.at[slot, k]).wait_recv()
 
-                @pl.when(either(far, handed))
+                @pl.when(k < handed)
                 def _():
                     pltpu.make_async_remote_copy(
                         src_ref=spot, dst_ref=spot, send_sem=relay_sem, recv_sem=take_sem,
@@ -268,33 +305,41 @@
     def rows_of(count):
         return out_ref.at[:, pl.ds(0, count * BLOCK), :]
 
+    def await_rows(count, sent, sem):
+        if count:
+            wait = span_bytes(rows_of(count), sem, sem)
+            (wait.wait_send if sent else wait.wait_recv)()
+
     for m in range(n):
-        cross_owners = [o for o in range(n) if (o < half) != (m < half)]
         near = [o for o in range(n) if (o < half) == (m < half)]
+        far = [o for o in range(n) if o not in near]
         into = near if m % 2 == 0 else list(range(n))
-        with_direct = [o for o in cross_owners if m % 2 == 0 and o not in DIRECT]
+        received = sum(sizes[o] for o in into)
+        relayed = sum(sizes[o] - direct_of[o] for o in far) if m % 2 == 0 else 0
 
         @pl.when(jnp.logical_and(me == m, leaf))
         def _():
-            span_bytes(outgoing, send_sem, take_sem).wait_send()
-            span_bytes(rows_of(sum(sizes[o] for o in into)), give_sem, take_sem).wait_recv()
+            span_bytes(outgoing, send_sem, send_sem).wait_send()
+            await_rows(received, False, take_sem)
 
         @pl.when(jnp.logical_and(me == m, hub))
         def _():
-            span_bytes(outgoing.at[pl.ds(0, blocks - sizes[m])], send_sem, take_sem).wait_send()
-            span_bytes(rows_of(sum(sizes[o] for o in into) - sizes[m]), give_sem, take_sem).wait_recv()
-            for _ in range(7 if m in DIRECT else 5):
-                span_bytes(rows_of(sizes[m]), give_sem, take_sem).wait_send()
-        if with_direct:
+            span_bytes(outgoing.at[pl.ds(0, blocks - sizes[m])], send_sem, send_sem).wait_send()
+            await_rows(received - sizes[m], False, take_sem)
+            for _ in range(5):
+                await_rows(sizes[m], True, give_sem)
+            for _ in range(2):
+                await_rows(direct_of[m], True, give_sem)
+        if relayed:
             @pl.when(me == m)
             def _():
-                span_bytes(rows_of(sum(sizes[o] for o in with_direct)), relay_sem, take_sem).wait_send()
+                await_rows(relayed, True, relay_sem)
 
 
 def fused_call(emissivity, bin_index, color_table, brick_order, n, ray_step):
     cells, cols_x, cols_y = emissivity.shape
     blocks = cols_x // BLOCK
-    most = max(owned_sizes(blocks))
+    most = max(scaled(SIZES, blocks))
     return pl.pallas_call(
         functools.partial(fused, n, ray_step),
         out_shape=pltpu.VMEM((4, cols_x, cols_y), jnp.float32),
@@ -317,6 +362,8 @@
             pltpu.SemaphoreType.DMA((2, most)),
             pltpu.SemaphoreType.DMA(()),
             pltpu.SemaphoreType.REGULAR,
+            pltpu.SemaphoreType.REGULAR((n,)),
+            pltpu.SemaphoreType.REGULAR,
         ],
         compiler_params=pltpu.CompilerParams(collective_id=0, has_side_effects=True),
     )(emissivity, bin_index, color_table, brick_order)
@@ -358,7 +405,7 @@
     n = lax.axis_size("depth")
     ray_step = 2.0 / (cells * n)
     paired = lax.axis_size("imgx") % 2 == 0
-    piecewise = n == len(RS) and paired and cols_x % (4 * n * BLOCK) == 0
+    piecewise = n == len(RS) and paired and cols_x % (sum(SIZES) * BLOCK) == 0
     form = fused_call if piecewise else spread
     return form(emissivity, bin_index, color_table, brick_order, n, ray_step)
 

time: 17 us -> 16.6 us (0.976)
  Pallas kernels: 16.1 us -> 15.7 us
    pallas_call x1, Pallas kernels: 16.1 us -> 15.7 us  [fused_call(): pl.pallas_call(functools.partial(fused, n, ray_step), out_shape=pltpu.VME...]
where the time goes in v2:
time: 16.6 us; the launch traced here: 16.4 us
  Pallas kernels  15.7 us (95%)
  local copies, waits for them, and re-layouts  0.71 us (4%)
    pallas_call x1, Pallas kernels, fused_call(): pl.pallas_call(functools.partial(fused, n, ray_step), out_shape=pltpu.VME...  15.7 us
    unnamed x1, local copies, waits for them, and re-layouts  0.71 us

profile of v2, /device:TPU:0, one launch (start us, length us, event | category | flops | bytes accessed | tf_op | source)
XLA Modules:
  0.0 16.4 jit_solution(14633890394068313674)
XLA Ops:
  0.0 15.7 %shard_map.46 = f32[4,128,128]{2,1,0:T(8,128)S(1)} custom-call(bf16[8,128,128]{2,1,0:T(8,128)(2,1)} %emis_hbm.1, s32[8,128,128]{2,1,0:T(8,128)} %bins_hbm.1, bf16[4,128]{1,0:T(4,128)(2,1)} %table_in.1, s32[4]{0:T(128)} %order_in.1), custom_call_target="tpu_custom_call" | custom-call | tf_op jit(solution)/shard_map/pallas_call | solution.py:343
  15.7 0.7 %copy.6 = f32[4,128,128]{2,1,0:T(8,128)} copy(f32[4,128,128]{2,1,0:T(8,128)S(1)} %shard_map.46) | data formatting | bytes 524288

commit v3 on v2

--- a/solution.py
+++ b/solution.py
@@ -11,9 +11,9 @@
 BLOCK = 8
 LANES = 128
 MEET = 12
-GROUP = 4
-RS = (((1,), (2,), (3,), (0,)), ((0,), (2,), (3,), (1,)), ((0, 1), (3,), (2,)), ((2, 0, 1), (3,)))
-RELAY_ORDER = ((3, 0), (2, 1))
+GROUP = 2
+RS = (((1, 0, 0.33), (2, 0.34, 1), (0, 2, 3)), ((0, 0, 0.18), (2, 0.34, 1), (1, 2, 3)), ((0, 0, 1), (1, 0, 1), (3, 1, 1.5), (2, 2, 3)), ((0, 0, 1), (1, 0, 0.7), (2, 0, 1), (3, 2, 3)))
+RELAY_ORDER = ((2, 0), (3, 1))
 DIRECT = (1, 1, 4, 0)
 SIZES = (4, 4, 8, 0)
 
@@ -73,12 +73,9 @@
     return tuple(share * blocks // sum(SIZES) for share in shares)
 
 
-def owned_blocks(sizes, groups):
-    steps = []
-    for group in groups:
-        woven = [((k + 0.5) / sizes[o], i, o, k) for i, o in enumerate(group) for k in range(sizes[o])]
-        steps += [(o, k) for _, _, o, k in sorted(woven)]
-    return steps
+def owned_blocks(sizes, spans):
+    steps = [(begin + (end - begin) * (k + 0.5) / sizes[o], o, k) for o, begin, end in spans for k in range(sizes[o])]
+    return [(o, k) for _, o, k in sorted(steps)]
 
 
 def either(me, members):
@@ -86,8 +83,8 @@
 
 
 def fused(n, ray_step, emis_hbm, bins_hbm, table_in, order_in, out_ref,
-          emis, bins, outgoing, arrived, mine, table_v, order_s, in_sem, aux_sem,
-          send_sem, recv_sem, give_sem, take_sem, cross_sem, relay_sem, ready_sem, know_sem, leaf_sem):
+          emis, bins, outgoing, arrived, mine, table_v, order_s, in_sem,
+          out_sem, recv_sem, take_sem, cross_sem, ready_sem, know_sem):
     me = lax.axis_index("depth")
     y = lax.axis_index("imgx")
     core = lax.rem(y, 2)
@@ -126,13 +123,23 @@
 
     for q in range(blocks):
         src = block_rows(block[q])
-        pltpu.make_async_copy(emis_hbm.at[:, src, :], emis.at[q], in_sem.at[0, q // group]).start()
-        pltpu.make_async_copy(bins_hbm.at[:, src, :], bins.at[q], in_sem.at[1, q // group]).start()
+        pltpu.make_async_copy(emis_hbm.at[:, src, :], emis.at[q], in_sem.at[q // group]).start()
+        pltpu.make_async_copy(bins_hbm.at[:, src, :], bins.at[q], in_sem.at[q // group]).start()
         if q == group - 1:
-            tc = pltpu.make_async_copy(table_in, table_v, aux_sem.at[0])
-            oc = pltpu.make_async_copy(order_in, order_s, aux_sem.at[1])
+            tc = pltpu.make_async_copy(table_in, table_v, in_sem.at[0])
             tc.start()
-            oc.start()
+    oc = pltpu.make_async_copy(order_in, order_s, in_sem.at[GROUP - 1])
+    oc.start()
+
+    def await_group(g):
+        part = pl.ds(g * group, group)
+        pltpu.make_async_copy(emis.at[part], emis.at[part], in_sem.at[g]).wait()
+        pltpu.make_async_copy(bins.at[part], bins.at[part], in_sem.at[g]).wait()
+        if g == 0:
+            tc.wait()
+        if g == GROUP - 1:
+            oc.wait()
+
     pl.semaphore_wait(barrier, jnp.where(hub, jnp.maximum(me, 1), 1))
 
     @pl.when(hub)
@@ -141,7 +148,7 @@
             @pl.when(d < me)
             def _():
                 pl.semaphore_signal(know_sem.at[me], inc=1, device_id=at_hub(d), device_id_type=MESH)
-        pl.semaphore_wait(leaf_sem, 1)
+        pl.semaphore_wait(know_sem.at[me], 1)
         for d in range(n):
             @pl.when(d < me)
             def _():
@@ -149,7 +156,7 @@
 
     @pl.when(leaf)
     def _():
-        pl.semaphore_signal(leaf_sem, inc=1, device_id=at_hub(me), device_id_type=MESH)
+        pl.semaphore_signal(know_sem.at[me], inc=1, device_id=at_hub(me), device_id_type=MESH)
 
     def meet(t):
         @pl.when(jnp.logical_and(hub, t > me))
@@ -161,25 +168,24 @@
         def _():
             pl.semaphore_wait(know_sem.at[t], 1)
 
-    tc.wait()
+    await_group(0)
     tables = scaled_tables(table_v, ray_step)
 
     def ship(q):
         pltpu.make_async_remote_copy(
             src_ref=outgoing.at[q],
-            dst_ref=arrived.at[core, place[q], me],
-            send_sem=send_sem,
-            recv_sem=recv_sem.at[core, place[q]],
+            dst_ref=arrived.at[place[q], core * n + me],
+            send_sem=out_sem,
+            recv_sem=recv_sem.at[place[q]],
             device_id=at_hub(owner[q]),
             device_id_type=MESH,
         ).start()
 
-    last_meet = blocks * MEET // sum(SIZES)
+    met = [next(q for q in range(blocks) if plan[m][q][0] == o) for m in range(n) for o in range(n) if o != m and sizes[o]]
+    last_meet = max(blocks * MEET // sum(SIZES), *met)
     for q in range(blocks):
-        if q % group == 0:
-            part = pl.ds(q, group)
-            pltpu.make_async_copy(emis.at[part], emis.at[part], in_sem.at[0, q // group]).wait()
-            pltpu.make_async_copy(bins.at[part], bins.at[part], in_sem.at[1, q // group]).wait()
+        if q % group == 0 and q:
+            await_group(q // group)
         got = march(tables, emis.at[q], bins.at[q], 0)
         for c in range(4):
             outgoing[q, c, :, :] = got[c]
@@ -207,17 +213,17 @@
 
             @pl.when(here)
             def _():
-                arrived[1, place[q], me] = outgoing[q]
+                arrived[place[q], n + me] = outgoing[q]
 
             @pl.when(jnp.logical_not(here))
             def _():
                 ship(q)
 
-    oc.wait()
     own_count = pick(sizes, me)
     cross = jnp.where(me < half, half, 0)
     partner = me + 1 - 2 * lax.rem(me, 2)
-    cross_slot = jnp.where(me < half, me, n - 1 - me)
+    cross_base = [offs[o] - offs[o // half * half] for o in range(n)]
+    cross_at = pick(cross_base, me)
     direct = pick(direct_of, me)
 
     def span_bytes(ref, sem, other):
@@ -227,7 +233,7 @@
         pltpu.make_async_remote_copy(
             src_ref=mine.at[tile, k],
             dst_ref=out_ref.at[:, block_rows(first_own + k), :],
-            send_sem=give_sem,
+            send_sem=out_sem,
             recv_sem=sem,
             device_id=at_leaf(d) if tile == 0 else at_hub(d),
             device_id_type=MESH,
@@ -240,8 +246,7 @@
         before = [[rank[a] < rank[b] for b in range(n)] for a in range(n)]
 
         def settle(k, tile):
-            span_bytes(arrived.at[tile, 0, pl.ds(0, n - tile)], send_sem, recv_sem.at[tile, k]).wait_recv()
-            passed = [arrived[tile, k, m, 3] for m in range(n)]
+            passed = [arrived[k, tile * n + m, 3] for m in range(n)]
             through = functools.reduce(lambda u, v: u * v, passed)
             color = [0.0] * 3
             for b in range(n):
@@ -250,15 +255,16 @@
                     if a != b:
                         factor = jnp.where(before[a][b], passed[a], 1.0)
                         ahead = factor if ahead is None else ahead * factor
-                color = [color[c] + ahead * arrived[tile, k, b, c] for c in range(3)]
+                color = [color[c] + ahead * arrived[k, tile * n + b, c] for c in range(3)]
             for c in range(3):
                 mine[tile, k, c] = color[c]
             mine[tile, k, 3] = 1.0 - through
 
         def chunk(k, carry):
+            span_bytes(arrived.at[0, pl.ds(0, 2 * n - 1)], out_sem, recv_sem.at[k]).wait_recv()
             for tile in range(2):
                 settle(k, tile)
-                give(k, tile, cross, cross_sem.at[cross_slot, k])
+                give(k, tile, cross, cross_sem.at[cross_at + k])
                 give(k, tile, partner, take_sem)
                 if tile == 0:
                     give(k, tile, me, take_sem)
@@ -286,17 +292,17 @@
             both = (left_far, right_far)
             begin = pick([offs[left_far]] * half + [offs[right_far]] * half, me)
             count = pick([sizes[left_far]] * half + [sizes[right_far]] * half, me)
-            slot = pick([n - 1 - left_far] * half + [right_far] * half, me)
+            slot = pick([cross_base[left_far]] * half + [cross_base[right_far]] * half, me)
             handed = count - pick([direct_of[left_far]] * half + [direct_of[right_far]] * half, me)
 
             def relay(k, carry):
                 spot = out_ref.at[:, block_rows(begin + k), :]
-                span_bytes(spot, relay_sem, cross_sem.at[slot, k]).wait_recv()
+                span_bytes(spot, out_sem, cross_sem.at[slot + k]).wait_recv()
 
                 @pl.when(k < handed)
                 def _():
                     pltpu.make_async_remote_copy(
-                        src_ref=spot, dst_ref=spot, send_sem=relay_sem, recv_sem=take_sem,
+                        src_ref=spot, dst_ref=spot, send_sem=out_sem, recv_sem=take_sem,
                         device_id={"depth": me + 1}, device_id_type=MESH).start()
                 return carry
 
@@ -305,41 +311,36 @@
     def rows_of(count):
         return out_ref.at[:, pl.ds(0, count * BLOCK), :]
 
-    def await_rows(count, sent, sem):
-        if count:
-            wait = span_bytes(rows_of(count), sem, sem)
-            (wait.wait_send if sent else wait.wait_recv)()
-
-    for m in range(n):
+    def await_sent(count):
+        while count > 0:
+            span_bytes(rows_of(min(count, blocks)), out_sem, out_sem).wait_send()
+            count -= blocks
+
+    for m in reversed(range(n)):
         near = [o for o in range(n) if (o < half) == (m < half)]
         far = [o for o in range(n) if o not in near]
         into = near if m % 2 == 0 else list(range(n))
         received = sum(sizes[o] for o in into)
         relayed = sum(sizes[o] - direct_of[o] for o in far) if m % 2 == 0 else 0
 
+        @pl.when(jnp.logical_and(me == m, hub))
+        def _():
+            await_sent(blocks + 4 * sizes[m] + 2 * direct_of[m] + relayed)
+            if received > sizes[m]:
+                span_bytes(rows_of(received - sizes[m]), take_sem, take_sem).wait_recv()
+
         @pl.when(jnp.logical_and(me == m, leaf))
         def _():
-            span_bytes(outgoing, send_sem, send_sem).wait_send()
-            await_rows(received, False, take_sem)
-
-        @pl.when(jnp.logical_and(me == m, hub))
-        def _():
-            span_bytes(outgoing.at[pl.ds(0, blocks - sizes[m])], send_sem, send_sem).wait_send()
-            await_rows(received - sizes[m], False, take_sem)
-            for _ in range(5):
-                await_rows(sizes[m], True, give_sem)
-            for _ in range(2):
-                await_rows(direct_of[m], True, give_sem)
-        if relayed:
-            @pl.when(me == m)
-            def _():
-                await_rows(relayed, True, relay_sem)
+            await_sent(blocks + relayed)
+            span_bytes(rows_of(received), take_sem, take_sem).wait_recv()
 
 
 def fused_call(emissivity, bin_index, color_table, brick_order, n, ray_step):
     cells, cols_x, cols_y = emissivity.shape
     blocks = cols_x // BLOCK
-    most = max(scaled(SIZES, blocks))
+    sizes = scaled(SIZES, blocks)
+    most = max(sizes)
+    crossing = max(sum(sizes[: n // 2]), sum(sizes[n // 2 :]))
     return pl.pallas_call(
         functools.partial(fused, n, ray_step),
         out_shape=pltpu.VMEM((4, cols_x, cols_y), jnp.float32),
@@ -349,21 +350,17 @@
             pltpu.VMEM((blocks, cells, BLOCK, cols_y), jnp.bfloat16),
             pltpu.VMEM((blocks, cells, BLOCK, cols_y), jnp.int32),
             pltpu.VMEM((blocks, 4, BLOCK, cols_y), jnp.float32),
-            pltpu.VMEM((2, most, n, 4, BLOCK, cols_y), jnp.float32),
+            pltpu.VMEM((most, 2 * n, 4, BLOCK, cols_y), jnp.float32),
             pltpu.VMEM((2, most, 4, BLOCK, cols_y), jnp.float32),
             pltpu.VMEM(color_table.shape, color_table.dtype),
             pltpu.SMEM(brick_order.shape, brick_order.dtype),
-            pltpu.SemaphoreType.DMA((2, GROUP)),
-            pltpu.SemaphoreType.DMA((2,)),
+            pltpu.SemaphoreType.DMA((GROUP,)),
             pltpu.SemaphoreType.DMA(()),
-            pltpu.SemaphoreType.DMA((2, most)),
+            pltpu.SemaphoreType.DMA((most,)),
             pltpu.SemaphoreType.DMA(()),
-            pltpu.SemaphoreType.DMA(()),
-            pltpu.SemaphoreType.DMA((2, most)),
-            pltpu.SemaphoreType.DMA(()),
+            pltpu.SemaphoreType.DMA((crossing,)),
             pltpu.SemaphoreType.REGULAR,
             pltpu.SemaphoreType.REGULAR((n,)),
-            pltpu.SemaphoreType.REGULAR,
         ],
         compiler_params=pltpu.CompilerParams(collective_id=0, has_side_effects=True),
     )(emissivity, bin_index, color_table, brick_order)

time: 16.6 us -> 16.1 us (0.970)
  Pallas kernels: 15.7 us -> 15.2 us
    pallas_call x1, Pallas kernels: 15.7 us -> 15.2 us  [fused_call(): pl.pallas_call(functools.partial(fused, n, ray_step), out_shape=pltpu.VME...]
where the time goes in v3:
time: 16.1 us; the launch traced here: 15.9 us
  Pallas kernels  15.2 us (94%)
  local copies, waits for them, and re-layouts  0.71 us (4%)
    pallas_call x1, Pallas kernels, fused_call(): pl.pallas_call(functools.partial(fused, n, ray_step), out_shape=pltpu.VME...  15.2 us
    unnamed x1, local copies, waits for them, and re-layouts  0.71 us

profile of v3, /device:TPU:0, one launch (start us, length us, event | category | flops | bytes accessed | tf_op | source)
XLA Modules:
  0.0 15.9 jit_solution(14240853334830528191)
XLA Ops:
  0.0 15.2 %shard_map.46 = f32[4,128,128]{2,1,0:T(8,128)S(1)} custom-call(bf16[8,128,128]{2,1,0:T(8,128)(2,1)} %emis_hbm.1, s32[8,128,128]{2,1,0:T(8,128)} %bins_hbm.1, bf16[4,128]{1,0:T(4,128)(2,1)} %table_in.1, s32[4]{0:T(128)} %order_in.1), custom_call_target="tpu_custom_call" | custom-call | tf_op jit(solution)/shard_map/pallas_call | solution.py:344
  15.2 0.7 %copy.6 = f32[4,128,128]{2,1,0:T(8,128)} copy(f32[4,128,128]{2,1,0:T(8,128)S(1)} %shard_map.46) | data formatting | bytes 524288

commit v4 on v3

--- a/solution.py
+++ b/solution.py
@@ -12,9 +12,14 @@
 LANES = 128
 MEET = 12
 GROUP = 2
-RS = (((1, 0, 0.33), (2, 0.34, 1), (0, 2, 3)), ((0, 0, 0.18), (2, 0.34, 1), (1, 2, 3)), ((0, 0, 1), (1, 0, 1), (3, 1, 1.5), (2, 2, 3)), ((0, 0, 1), (1, 0, 0.7), (2, 0, 1), (3, 2, 3)))
-RELAY_ORDER = ((2, 0), (3, 1))
-DIRECT = (1, 1, 4, 0)
+RS = (
+    ((1, 0, 0.6), (2, 0.2, 1), (0, 2, 3)),
+    ((2, 0, 0.9), (0, 0.5, 1), (1, 2, 3)),
+    ((0, 0, 1), (1, 0, 1), (3, 1, 1.5), (2, 2, 3)),
+    ((0, 0, 1), (1, 0, 0.7), (2, 0, 1), (3, 2, 3)),
+)
+RELAY_ORDER = ((2, 1), (3, 0))
+DIRECT = (1, 0, 4, 0)
 SIZES = (4, 4, 8, 0)
 
 

time: 16.1 us -> 15.9 us (0.988)
  Pallas kernels: 15.2 us -> 15 us
    pallas_call x1, Pallas kernels: 15.2 us -> 15 us  [fused_call(): pl.pallas_call(functools.partial(fused, n, ray_step), out_shape=pltpu.VME...]
where the time goes in v4:
time: 15.9 us; the launch traced here: 15.7 us
  Pallas kernels  15 us (94%)
  local copies, waits for them, and re-layouts  0.71 us (4%)
    pallas_call x1, Pallas kernels, fused_call(): pl.pallas_call(functools.partial(fused, n, ray_step), out_shape=pltpu.VME...  15 us
    unnamed x1, local copies, waits for them, and re-layouts  0.71 us

profile of v4, /device:TPU:0, one launch (start us, length us, event | category | flops | bytes accessed | tf_op | source)
XLA Modules:
  0.0 15.7 jit_solution(16208310832401380036)
XLA Ops:
  0.0 15.0 %shard_map.46 = f32[4,128,128]{2,1,0:T(8,128)S(1)} custom-call(bf16[8,128,128]{2,1,0:T(8,128)(2,1)} %emis_hbm.1, s32[8,128,128]{2,1,0:T(8,128)} %bins_hbm.1, bf16[4,128]{1,0:T(4,128)(2,1)} %table_in.1, s32[4]{0:T(128)} %order_in.1), custom_call_target="tpu_custom_call" | custom-call | tf_op jit(solution)/shard_map/pallas_call | solution.py:349
  15.0 0.7 %copy.6 = f32[4,128,128]{2,1,0:T(8,128)} copy(f32[4,128,128]{2,1,0:T(8,128)S(1)} %shard_map.46) | data formatting | bytes 524288

commit v5 on v4

--- a/solution.py
+++ b/solution.py
@@ -19,7 +19,7 @@
     ((0, 0, 1), (1, 0, 0.7), (2, 0, 1), (3, 2, 3)),
 )
 RELAY_ORDER = ((2, 1), (3, 0))
-DIRECT = (1, 0, 4, 0)
+DIRECT = (2, 0, 4, 0)
 SIZES = (4, 4, 8, 0)
 
 
@@ -269,7 +269,7 @@
             span_bytes(arrived.at[0, pl.ds(0, 2 * n - 1)], out_sem, recv_sem.at[k]).wait_recv()
             for tile in range(2):
                 settle(k, tile)
-                give(k, tile, cross, cross_sem.at[cross_at + k])
+                give(k, tile, cross, cross_sem.at[lax.div(cross_at + k, 2)])
                 give(k, tile, partner, take_sem)
                 if tile == 0:
                     give(k, tile, me, take_sem)
@@ -301,17 +301,17 @@
             handed = count - pick([direct_of[left_far]] * half + [direct_of[right_far]] * half, me)
 
             def relay(k, carry):
-                spot = out_ref.at[:, block_rows(begin + k), :]
-                span_bytes(spot, out_sem, cross_sem.at[slot + k]).wait_recv()
-
-                @pl.when(k < handed)
+                spot = out_ref.at[:, pl.ds(pl.multiple_of((begin + 2 * k) * BLOCK, BLOCK), 2 * BLOCK), :]
+                span_bytes(spot, out_sem, cross_sem.at[lax.div(slot, 2) + k]).wait_recv()
+
+                @pl.when(2 * k < handed)
                 def _():
                     pltpu.make_async_remote_copy(
                         src_ref=spot, dst_ref=spot, send_sem=out_sem, recv_sem=take_sem,
                         device_id={"depth": me + 1}, device_id_type=MESH).start()
                 return carry
 
-            lax.fori_loop(0, count, relay, 0)
+            lax.fori_loop(0, lax.div(count, 2), relay, 0)
 
     def rows_of(count):
         return out_ref.at[:, pl.ds(0, count * BLOCK), :]
@@ -363,7 +363,7 @@
             pltpu.SemaphoreType.DMA(()),
             pltpu.SemaphoreType.DMA((most,)),
             pltpu.SemaphoreType.DMA(()),
-            pltpu.SemaphoreType.DMA((crossing,)),
+            pltpu.SemaphoreType.DMA((crossing // 2,)),
             pltpu.SemaphoreType.REGULAR,
             pltpu.SemaphoreType.REGULAR((n,)),
         ],

time: 15.9 us -> 16.2 us (1.019)
  the two profiles are of different devices: /device:TPU:0 before, /device:TPU:1 now
where the time goes in v5:
time: 16.2 us; the launch traced here: 16 us
  Pallas kernels  15.3 us (94%)
  local copies, waits for them, and re-layouts  0.71 us (4%)
    pallas_call x1, Pallas kernels, fused_call(): pl.pallas_call(functools.partial(fused, n, ray_step), out_shape=pltpu.VME...  15.3 us
    unnamed x1, local copies, waits for them, and re-layouts  0.71 us

profile of v5, /device:TPU:1, one launch (start us, length us, event | category | flops | bytes accessed | tf_op | source)
XLA Modules:
  0.0 16.0 jit_solution(4235499548573737138)
XLA Ops:
  0.0 15.3 %shard_map.46 = f32[4,128,128]{2,1,0:T(8,128)S(1)} custom-call(bf16[8,128,128]{2,1,0:T(8,128)(2,1)} %emis_hbm.1, s32[8,128,128]{2,1,0:T(8,128)} %bins_hbm.1, bf16[4,128]{1,0:T(4,128)(2,1)} %table_in.1, s32[4]{0:T(128)} %order_in.1), custom_call_target="tpu_custom_call" | custom-call | tf_op jit(solution)/shard_map/pallas_call | solution.py:349
  15.3 0.7 %copy.6 = f32[4,128,128]{2,1,0:T(8,128)} copy(f32[4,128,128]{2,1,0:T(8,128)S(1)} %shard_map.46) | data formatting | bytes 524288
